TPU v7x, 32 devices: a whole 2x2x4 slice. The times are simulated.
32 devices in a mesh: req: 2 (over y), patch: 16 (over z, x, core).
Axes of the slice: x: 2, y: 2, z: 4, core: 2. Of those that a mesh axis runs over, the one named last changes fastest.
Arguments:
- tokens: bfloat16 [1536, 1152], P(('req', 'patch')), parts along dimension 0, may hold values from -6 to 6
- positions: int32 [2, 1536], P(None, ('req', 'patch')), parts along dimension 1, may hold values from 0 to 95
- counts: int32 [32], P('req'), parts along dimension 0, may hold values from 1 to 48, 384 in all
- timestep: int32 [2], P('req'), parts along dimension 0, may hold values from 0 to 999
- time_in: bfloat16 [256, 1152], replicated, may hold values from -0.375 to 0.375
- time_out: bfloat16 [1152, 1152], P(None, 'patch'), may hold values from -0.1875 to 0.1875
- ada_weight: bfloat16 [1152, 3456], P('patch'), may hold values from -0.375 to 0.375
- qkv_weight: bfloat16 [1152, 3456], replicated, may hold values from -2 to 2, as said below
- out_weight: bfloat16 [1152, 1152], replicated, may hold values from -0.1875 to 0.1875
Outputs:
- block_out: bfloat16 [1536, 1152], P(('req', 'patch')), parts along dimension 0
There are 2 independent parts, one for each index of `req`. A program takes and returns all parts, laid end to end along the dimension named above; an argument that names none is the same for every part. Nothing has to cross between parts.
Inputs may be any that keep to these rules, and one draw needn't show every extreme that they name: `counts`: used slots are the first ones of each block; they sum to exactly 384, and some block uses all 48. `qkv_weight`: columns are 1152 of queries, 1152 of keys, 1152 of values, each head's 72 columns side by side.
All inputs are finite; a program needn't handle non-finite values.
Results may differ from a plain program's by a relative error of at most 0.0039.
Values may be sent and summed in bfloat16 or wider, within the bound.
A program may use at most 64 MiB of HBM per device.

v0:
```python
import math
import jax
import jax.numpy as jnp
from jax import lax
from jax.sharding import PartitionSpec as P

HEADS = 16
neg_large = -1e30
key_block = 512


def time_features(timestep, freq_size):
    half_size = freq_size // 2
    frequencies = jnp.exp(-math.log(10000.0) * jnp.arange(half_size, dtype=jnp.float32) / half_size)
    angles = timestep.astype(jnp.float32)[:, None] * frequencies[None, :]
    return jnp.concatenate([jnp.cos(angles), jnp.sin(angles)], axis=1).astype(jnp.bfloat16)


def position_table(positions, model_width):
    quarter = model_width // 4
    omegas = jnp.power(10000.0, -jnp.arange(quarter, dtype=jnp.float32) / quarter)
    row_angle = positions[0].astype(jnp.float32)[:, None] * omegas[None, :]
    col_angle = positions[1].astype(jnp.float32)[:, None] * omegas[None, :]
    return jnp.concatenate(
        [jnp.sin(row_angle), jnp.cos(row_angle), jnp.sin(col_angle), jnp.cos(col_angle)], axis=1
    )


def attend_update(running, query_heads, key_piece, value_piece, mask_piece, inv_root):
    row_top, denominator, weighted = running
    key_count = key_piece.shape[0]
    head_count = query_heads.shape[1]
    head_size = query_heads.shape[2]
    key_heads = key_piece.reshape(key_count, head_count, head_size)
    value_heads = value_piece.reshape(key_count, head_count, head_size)
    scores = (
        jnp.einsum("qhd,khd->hqk", query_heads, key_heads, preferred_element_type=jnp.float32)
        * inv_root
    )
    scores = jnp.where(mask_piece[None, None, :], scores, neg_large)
    new_top = jnp.maximum(row_top, jnp.max(scores, axis=2))
    weights = jnp.where(mask_piece[None, None, :], jnp.exp(scores - new_top[:, :, None]), 0.0)
    factor = jnp.exp(row_top - new_top)
    denominator = denominator * factor + jnp.sum(weights, axis=2)
    rounded = weights.astype(jnp.bfloat16)
    weighted = weighted * factor[:, :, None] + jnp.einsum(
        "hqk,khd->hqd", rounded, value_heads, preferred_element_type=jnp.float32
    )
    return (new_top, denominator, weighted)


def make_folder(query_heads, key_valid, inv_root):

    def fold_keys(running, shard_piece, start_row):
        key_piece, value_piece = shard_piece
        key_count = key_piece.shape[0]
        if key_count > 2 * key_block and key_count % key_block == 0:
            block_total = key_count // key_block

            def block_step(carried, block_items):
                return (
                    attend_update(
                        carried,
                        query_heads,
                        block_items[0],
                        block_items[1],
                        block_items[2],
                        inv_root,
                    ),
                    None,
                )

            stacked = (
                key_piece.reshape(block_total, key_block, key_piece.shape[1]),
                value_piece.reshape(block_total, key_block, value_piece.shape[1]),
                key_valid.reshape(block_total, key_block),
            )
            running, unused = lax.scan(block_step, running, stacked)
            return running
        return attend_update(running, query_heads, key_piece, value_piece, key_valid, inv_root)

    return fold_keys


def initial_state(query_rows, head_count, head_size):
    return (
        jnp.full((head_count, query_rows), neg_large, jnp.float32),
        jnp.zeros((head_count, query_rows), jnp.float32),
        jnp.zeros((head_count, query_rows, head_size), jnp.float32),
    )


def finish_state(running):
    row_top, denominator, weighted = running
    normalized = weighted / denominator[:, :, None]
    head_count, query_rows, head_size = normalized.shape
    return (
        jnp.transpose(normalized, (1, 0, 2))
        .reshape(query_rows, head_count * head_size)
        .astype(jnp.bfloat16)
    )


def per_device(
    tokens, positions, counts, timestep, time_in, time_out, ada_weight, qkv_weight, out_weight
):
    devices = lax.axis_size("patch")
    my_index = lax.axis_index("patch")
    local_rows = tokens.shape[0]
    model_width = tokens.shape[1]
    head_count = HEADS
    head_size = model_width // head_count
    inv_root = 1.0 / math.sqrt(head_size)
    features = time_features(timestep, time_in.shape[0])
    hidden_time = jax.nn.silu(
        jnp.dot(features, time_in, preferred_element_type=jnp.float32)
    ).astype(jnp.bfloat16)
    cond_part = jnp.dot(hidden_time, time_out, preferred_element_type=jnp.float32)
    activated = jax.nn.silu(cond_part).astype(jnp.bfloat16)
    partial_mod = jnp.dot(activated, ada_weight, preferred_element_type=jnp.float32)
    modulation = lax.psum(partial_mod, "patch")
    shift_mod = modulation[:, :model_width]
    scale_mod = modulation[:, model_width : 2 * model_width]
    gate_mod = modulation[:, 2 * model_width :]
    x_in = tokens.astype(jnp.float32) + position_table(positions, model_width)
    mean_value = jnp.mean(x_in, axis=1, keepdims=True)
    centered = x_in - mean_value
    variance = jnp.mean(centered * centered, axis=1, keepdims=True)
    normed = centered * lax.rsqrt(variance + 1e-06)
    modulated = (normed * (1.0 + scale_mod) + shift_mod).astype(jnp.bfloat16)
    counts_here = lax.dynamic_index_in_dim(counts, my_index, keepdims=False)
    row_ids = jnp.arange(local_rows, dtype=jnp.int32)
    row_valid = row_ids < counts_here
    projections = jnp.dot(modulated, qkv_weight, preferred_element_type=jnp.float32).astype(
        jnp.bfloat16
    )
    groups = devices // head_count
    part_rows = local_rows // groups
    query_split = projections[:, :model_width].reshape(groups, part_rows, head_count, head_size)
    query_send = jnp.transpose(query_split, (0, 2, 1, 3)).reshape(devices, part_rows, head_size)
    key_split = projections[:, model_width : 2 * model_width].reshape(
        local_rows, head_count, head_size
    )
    value_split = projections[:, 2 * model_width :].reshape(local_rows, head_count, head_size)
    pair_heads = jnp.transpose(jnp.concatenate([key_split, value_split], axis=2), (1, 0, 2))
    pair_send = jnp.broadcast_to(pair_heads[None], (groups, head_count, local_rows, 2 * head_size))
    pair_send = pair_send.reshape(devices, local_rows, 2 * head_size)
    got_query, got_pair = (
        lax.all_to_all(query_send, "patch", split_axis=0, concat_axis=0, tiled=True),
        lax.all_to_all(pair_send, "patch", split_axis=0, concat_axis=0, tiled=True),
    )
    query_rows = devices * part_rows
    query_heads = got_query.reshape(query_rows, 1, head_size)
    all_pairs = got_pair.reshape(devices * local_rows, 2 * head_size)
    key_valid = (jnp.arange(local_rows, dtype=jnp.int32)[None, :] < counts[:, None]).reshape(-1)
    folder = make_folder(query_heads, key_valid, inv_root)
    running = folder(
        initial_state(query_rows, 1, head_size),
        (all_pairs[:, :head_size], all_pairs[:, head_size:]),
        0,
    )
    head_result = finish_state(running).reshape(devices, part_rows, head_size)
    came_back = lax.all_to_all(head_result, "patch", split_axis=0, concat_axis=0, tiled=True)
    attended = jnp.transpose(
        came_back.reshape(groups, head_count, part_rows, head_size), (0, 2, 1, 3)
    )
    attended = attended.reshape(local_rows, model_width)
    projected = jnp.dot(attended, out_weight, preferred_element_type=jnp.float32)
    valid_column = row_valid.astype(jnp.float32)[:, None]
    return (x_in + gate_mod * projected * valid_column).astype(jnp.bfloat16)


def solution(mesh):
    placed = (
        P(("req", "patch"), None),
        P(None, ("req", "patch")),
        P("req"),
        P("req"),
        P(),
        P(None, "patch"),
        P("patch", None),
        P(),
        P(),
    )
    return jax.shard_map(
        per_device, mesh=mesh, in_specs=placed, out_specs=P(("req", "patch"), None), check_vma=False
    )
```

profile of v0, /device:TPU:0, one launch (start us, length us, event | category | flops | bytes accessed | tf_op | source)
XLA Modules:
  0.0 123.4 jit_solution(13335369351316423858)
XLA Ops:
  0.0 0.9 convert_bitcast_fusion
  1.6 1.0 fusion.25
  2.7 1.1 multiply_reduce_fusion
  4.5 1.3 %convolution_reduce_fusion = f32[1152]{0:T(1024)S(1)} fusion(bf16[256,1]{0,1:T(2,128)(2,1)S(1)} %reshape.180, bf16[256,1152]{1,0:T(8,128)(2,1)} %param.13), kind=kOutput, calls=%fused_computation.15 | convolution fusion | flops 589824 | bytes 594944 | tf_op jit(solution)/shard_map/dot_general | solution.py:116
  5.8 1.6 %fusion.27 = f32[1,3456]{1,0:T(1,128)S(1)} fusion(bf16[72,3456]{1,0:T(8,128)(2,1)} %param.15, bf16[1152,1]{0,1:T(2,128)(2,1)S(1)} %reshape.182, bf16[1152,72]{0,1:T(8,128)(2,1)} %param.14), kind=kOutput, calls=%fused_computation.46 | convolution fusion | flops 663912 | bytes 679680 | tf_op jit(solution)/shard_map/dot_general | solution.py:120
  7.4 63.0 %psum.7 = f32[1,3456]{1,0:T(1,128)S(1)} all-reduce(f32[1,3456]{1,0:T(1,128)S(1)} %fusion.27), channel_id=1, replica_groups=mesh['req'=2,'patch'=16] {'patch'}, use_global_device_ids=true, to_apply=%region_0.1 | all-reduce | flops 3456 | bytes 27648 | tf_op jit(solution)/shard_map/psum | solution.py:121
  70.4 4.6 %convolution_convert_fusion = bf16[48,3456]{1,0:T(8,128)(2,1)S(1)} fusion(bf16[1152,3456]{1,0:T(8,128)(2,1)} %param.16, f32[1152]{0:T(1024)S(1)} %get-tuple-element.6, f32[1152]{0:T(1024)S(1)} %get-tuple-element.7, f32[48]{0:T(128)S(1)} %add_rsqrt_fusion, f32[48]{0:T(128)S(1)} %broadcast_multiply_fusion, f32[48,1152]{1,0:T(8,128)S(1)} %concatenate.13, ...), kind=kOutput, calls=%fused_computation | convolution fusion | flops 382758912 | bytes 8635776 | tf_op jit(solution)/shard_map/dot_general | solution.py:134
  75.0 0.7 fusion.38
  76.1 0.7 copy.16
  76.8 3.5 %all-to-all-start = ((bf16[16,48,72]{2,1,0:T(8,128)(2,1)}), bf16[16,48,72]{2,1,0:T(8,128)(2,1)S(1)}, u32[]{:S(2)}, u32[]{:S(2)}) async-start(bf16[16,48,72]{2,1,0:T(8,128)(2,1)} %bitcast.38), calls=%async_computation | async-start | bytes 393216 | tf_op jit(solution)/shard_map/all_to_all | solution.py:149
  80.3 1.2 %reshape.175 = bf16[48,16,72]{2,1,0:T(8,128)(2,1)S(1)} reshape(bf16[48,1152]{1,0:T(8,128)(2,1)} %get-tuple-element.8) | data formatting | bytes 221184 | tf_op jit(solution)/shard_map/reshape | solution.py:141
  81.6 0.7 copy.11
  82.7 1.8 %maximum_bitcast_fusion = bf16[16,48,144]{2,1,0:T(8,128)(2,1)} fusion(bf16[48,16,72]{2,0,1:T(8,128)(2,1)S(1)} %copy.12, bf16[48,16,72]{2,0,1:T(8,128)(2,1)} %copy.11), kind=kLoop, calls=%fused_computation.17 | loop fusion | flops 442368 | bytes 442368 | tf_op jit(solution)/shard_map/transpose | solution.py:145
  84.5 4.7 %all-to-all-done = bf16[16,48,72]{2,1,0:T(8,128)(2,1)S(1)} async-done(((bf16[16,48,72]{2,1,0:T(8,128)(2,1)}), bf16[16,48,72]{2,1,0:T(8,128)(2,1)S(1)}, u32[]{:S(2)}, u32[]{:S(2)}) %all-to-all-start) | async-done | bytes 110624 | tf_op jit(solution)/shard_map/all_to_all | solution.py:149
  89.2 0.7 copy-done.2
  89.9 3.6 %all-to-all-start.1 = ((bf16[16,48,144]{2,1,0:T(8,128)(2,1)}), bf16[16,48,144]{2,1,0:T(8,128)(2,1)S(1)}, u32[]{:S(2)}, u32[]{:S(2)}) async-start(bf16[16,48,144]{2,1,0:T(8,128)(2,1)} %maximum_bitcast_fusion), calls=%async_computation.1 | async-start | bytes 786432 | tf_op jit(solution)/shard_map/all_to_all | solution.py:150
  93.6 12.0 %all-to-all-done.1 = bf16[16,48,144]{2,1,0:T(8,128)(2,1)S(1)} async-done(((bf16[16,48,144]{2,1,0:T(8,128)(2,1)}), bf16[16,48,144]{2,1,0:T(8,128)(2,1)S(1)}, u32[]{:S(2)}, u32[]{:S(2)}) %all-to-all-start.1) | async-done | bytes 221216 | tf_op jit(solution)/shard_map/all_to_all | solution.py:150
  105.6 1.5 %fusion.3 = (f32[768]{0:T(1024)S(1)}, f32[768,768]{0,1:T(8,128)S(1)}) fusion(pred[768]{0:T(1024)(128)(4,1)S(1)} %lt.37, bf16[768,72]{1,0:T(8,128)(2,1)} %bitcast.41, bf16[768,144]{1,0:T(8,128)(2,1)S(1)} %bitcast.39), kind=kOutput, calls=%fused_computation.7 | convolution fusion | flops 86703360 | bytes 2670592 | tf_op jit(solution)/shard_map/qhd,khd->hqk/dot_general | solution.py:37
  107.7 0.8 fusion.15
  108.6 0.8 copy.13
  109.4 3.5 %all-to-all-start.2 = ((bf16[16,48,72]{2,1,0:T(8,128)(2,1)}), bf16[16,48,72]{2,1,0:T(8,128)(2,1)S(1)}, u32[]{:S(2)}, u32[]{:S(2)}) async-start(bf16[16,48,72]{2,1,0:T(8,128)(2,1)} %bitcast.10), calls=%async_computation.2 | async-start | bytes 393216 | tf_op jit(solution)/shard_map/all_to_all | solution.py:163
  113.5 0.6 compare_convert_fusion
  114.1 7.7 %all-to-all-done.2 = bf16[16,48,72]{2,1,0:T(8,128)(2,1)S(1)} async-done(((bf16[16,48,72]{2,1,0:T(8,128)(2,1)}), bf16[16,48,72]{2,1,0:T(8,128)(2,1)S(1)}, u32[]{:S(2)}, u32[]{:S(2)}) %all-to-all-start.2) | async-done | bytes 110624 | tf_op jit(solution)/shard_map/all_to_all | solution.py:163
  122.1 1.2 %fusion.2 = bf16[48,1152]{1,0:T(8,128)(2,1)} fusion(bf16[48,1152]{1,0:T(8,128)(2,1)S(1)} %reshape.179, bf16[1152,1152]{1,0:T(8,128)(2,1)S(1)} %copy-done, f32[48]{0:T(128)S(1)} %compare_convert_fusion, f32[1152]{0:T(1024)S(1)} %get-tuple-element.5, f32[48,1152]{1,0:T(8,128)S(1)} %concatenate.13, bf16[48,1152]{1,0:T(8,128)(2,1)S(1)} %copy-done.1), kind=kOutput, calls=%fused_computation.6 | convolution fusion | flops 127733760 | bytes 3211968 | tf_op jit(solution)/shard_map/dot_general | solution.py:168
  (29 shorter events, 3.3 us)
Async XLA Ops:
  0.0 122.1 %copy-start = (bf16[1152,1152]{1,0:T(8,128)(2,1)S(1)}, bf16[1152,1152]{1,0:T(8,128)(2,1)}, u32[]{:S(2)}) copy-start(bf16[1152,1152]{1,0:T(8,128)(2,1)} %param.17) | copy-start | bytes 7962628
  0.0 70.4 %copy-start.1 = (bf16[48,1152]{1,0:T(8,128)(2,1)S(1)}, bf16[48,1152]{1,0:T(8,128)(2,1)}, u32[]{:S(2)}) copy-start(bf16[48,1152]{1,0:T(8,128)(2,1)} %param.9) | copy-start | bytes 331780
  75.0 18.4 %copy-start.3 = (s32[16]{0:T(128)S(1)}, s32[16]{0:T(128)}, u32[]{:S(2)}) copy-start(s32[16]{0:T(128)} %param.11) | copy-start | bytes 196
  76.8 12.5 %all-to-all-start = ((bf16[16,48,72]{2,1,0:T(8,128)(2,1)}), bf16[16,48,72]{2,1,0:T(8,128)(2,1)S(1)}, u32[]{:S(2)}, u32[]{:S(2)}) async-start(bf16[16,48,72]{2,1,0:T(8,128)(2,1)} %bitcast.38), calls=%async_computation | async-start | bytes 393216 | tf_op jit(solution)/shard_map/all_to_all | solution.py:149
  89.2 0.7 copy-start.2
  89.9 15.7 %all-to-all-start.1 = ((bf16[16,48,144]{2,1,0:T(8,128)(2,1)}), bf16[16,48,144]{2,1,0:T(8,128)(2,1)S(1)}, u32[]{:S(2)}, u32[]{:S(2)}) async-start(bf16[16,48,144]{2,1,0:T(8,128)(2,1)} %maximum_bitcast_fusion), calls=%async_computation.1 | async-start | bytes 786432 | tf_op jit(solution)/shard_map/all_to_all | solution.py:150
  109.4 12.5 %all-to-all-start.2 = ((bf16[16,48,72]{2,1,0:T(8,128)(2,1)}), bf16[16,48,72]{2,1,0:T(8,128)(2,1)S(1)}, u32[]{:S(2)}, u32[]{:S(2)}) async-start(bf16[16,48,72]{2,1,0:T(8,128)(2,1)} %bitcast.10), calls=%async_computation.2 | async-start | bytes 393216 | tf_op jit(solution)/shard_map/all_to_all | solution.py:163
where the time goes:
time: 124 us; the launch traced here: 123 us
  blocking collectives  63 us (51%)
  waiting for transfers between devices  24.3 us (20%)
  matrix products  11 us (9%)
  starting transfers between devices  10.6 us (9%)
  other arithmetic  6.94 us (6%)
  local copies, waits for them, and re-layouts  6.71 us (5%)
    psum x1, blocking collectives, per_device(): modulation = lax.psum(partial_mod, 'patch')  63 us
    all_to_all x1, waiting for transfers between devices, per_device(): lax.all_to_all(pair_send, 'patch', split_axis=0, concat_axis=0, tiled=True)  12 us
    all_to_all x1, waiting for transfers between devices, per_device(): lax.all_to_all(head_result, 'patch', split_axis=0, concat_axis=0, tiled=T...  7.68 us
    all_to_all x1, waiting for transfers between devices, per_device(): lax.all_to_all(query_send, 'patch', split_axis=0, concat_axis=0, tiled=True)  4.69 us
    dot_general x1, matrix products, per_device(): jnp.dot(modulated, qkv_weight, preferred_element_type=jnp.float32)  4.6 us
    all_to_all x1, starting transfers between devices, per_device(): lax.all_to_all(pair_send, 'patch', split_axis=0, concat_axis=0, tiled=True)  3.55 us
    all_to_all x1, starting transfers between devices, per_device(): lax.all_to_all(query_send, 'patch', split_axis=0, concat_axis=0, tiled=True)  3.52 us
    all_to_all x1, starting transfers between devices, per_device(): lax.all_to_all(head_result, 'patch', split_axis=0, concat_axis=0, tiled=T...  3.52 us
  transfers between devices with their start and end apart: 3, of which 3 were waited for; matrix products, arithmetic and copies ran while one was open for 5% of the time, Pallas kernels for 0%

commit v1 on v0

--- a/solution.py
+++ b/solution.py
@@ -118,7 +118,7 @@
     cond_part = jnp.dot(hidden_time, time_out, preferred_element_type=jnp.float32)
     activated = jax.nn.silu(cond_part).astype(jnp.bfloat16)
     partial_mod = jnp.dot(activated, ada_weight, preferred_element_type=jnp.float32)
-    modulation = lax.psum(partial_mod, "patch")
+    modulation = jnp.sum(lax.all_gather(partial_mod, "patch"), axis=0)
     shift_mod = modulation[:, :model_width]
     scale_mod = modulation[:, model_width : 2 * model_width]
     gate_mod = modulation[:, 2 * model_width :]

time: 124 us -> 84.9 us (0.68)
  blocking collectives: 63 us -> 23.7 us
    psum x1 -> x0, blocking collectives: 63 us -> none  [per_device(): modulation = lax.psum(partial_mod, 'patch')]
    all_gather x0 -> x1, blocking collectives: none -> 23.7 us  [per_device(): modulation = jnp.sum(lax.all_gather(partial_mod, 'patch'), axis=0)]
  transfers between devices with their start and end apart: 3 -> 3, of which waited for: 3 -> 3; matrix products, arithmetic and copies ran while one was open for 5% -> 7% of each run, Pallas kernels for 0% -> 0%
where the time goes in v1:
time: 84.9 us; the launch traced here: 84.3 us
  waiting for transfers between devices  24.3 us (29%)
  blocking collectives  23.7 us (28%)
  matrix products  11 us (13%)
  starting transfers between devices  10.6 us (12%)
  other arithmetic  7.09 us (8%)
  local copies, waits for them, and re-layouts  6.72 us (8%)
  between operations  0.88 us (1%)
    all_gather x1, blocking collectives, per_device(): modulation = jnp.sum(lax.all_gather(partial_mod, 'patch'), axis=0)  23.7 us
    all_to_all x1, waiting for transfers between devices, per_device(): lax.all_to_all(pair_send, 'patch', split_axis=0, concat_axis=0, tiled=True)  12 us
    all_to_all x1, waiting for transfers between devices, per_device(): lax.all_to_all(head_result, 'patch', split_axis=0, concat_axis=0, tiled=T...  7.68 us
    all_to_all x1, waiting for transfers between devices, per_device(): lax.all_to_all(query_send, 'patch', split_axis=0, concat_axis=0, tiled=True)  4.69 us
    dot_general x1, matrix products, per_device(): jnp.dot(modulated, qkv_weight, preferred_element_type=jnp.float32)  4.61 us
    all_to_all x1, starting transfers between devices, per_device(): lax.all_to_all(pair_send, 'patch', split_axis=0, concat_axis=0, tiled=True)  3.55 us
    all_to_all x1, starting transfers between devices, per_device(): lax.all_to_all(query_send, 'patch', split_axis=0, concat_axis=0, tiled=True)  3.52 us
    all_to_all x1, starting transfers between devices, per_device(): lax.all_to_all(head_result, 'patch', split_axis=0, concat_axis=0, tiled=T...  3.52 us
  transfers between devices with their start and end apart: 3, of which 3 were waited for; matrix products, arithmetic and copies ran while one was open for 7% of the time, Pallas kernels for 0%

profile of v1, /device:TPU:0, one launch (start us, length us, event | category | flops | bytes accessed | tf_op | source)
XLA Modules:
  0.0 84.3 jit_solution(7440912104920625258)
XLA Ops:
  0.0 0.9 %convert_bitcast_fusion = (f32[48]{0:T(128)S(1)}, f32[48]{0:T(128)S(1)}) fusion(s32[2,48]{1,0:T(2,128)} %param.10), kind=kLoop, calls=%fused_computation.55 | loop fusion | flops 96 | bytes 768 | tf_op jit(solution)/shard_map/convert_element_type | solution.py:23
  1.6 1.0 %fusion.25 = f32[48]{0:T(128)S(1)} fusion(f32[48,1152]{1,0:T(8,128)S(1)} %concatenate.13, bf16[48,1152]{1,0:T(8,128)(2,1)} %param.9), kind=kLoop, calls=%fused_computation.34 | loop fusion | flops 165840 | bytes 331968 | tf_op jit(solution)/shard_map/reduce_sum | solution.py:126
  2.7 1.1 %multiply_reduce_fusion = f32[48]{0:T(128)S(1)} fusion(f32[48]{0:T(128)S(1)} %broadcast_multiply_fusion, f32[48,1152]{1,0:T(8,128)S(1)} %concatenate.13, bf16[48,1152]{1,0:T(8,128)(2,1)} %param.9), kind=kLoop, calls=%fused_computation.20 | loop fusion | flops 276432 | bytes 332160 | tf_op jit(solution)/shard_map/reduce_sum | solution.py:128
  4.5 1.3 %convolution_reduce_fusion = f32[1152]{0:T(1024)S(1)} fusion(bf16[256,1]{0,1:T(2,128)(2,1)S(1)} %reshape.187, bf16[256,1152]{1,0:T(8,128)(2,1)} %param.13), kind=kOutput, calls=%fused_computation.16 | convolution fusion | flops 589824 | bytes 594944 | tf_op jit(solution)/shard_map/dot_general | solution.py:116
  5.8 1.6 %convolution_bitcast_fusion = f32[1,1,3456]{2,1,0:T(1,128)S(1)} fusion(bf16[72,3456]{1,0:T(8,128)(2,1)} %param.15, bf16[1152,1]{0,1:T(2,128)(2,1)S(1)} %reshape.189, bf16[1152,72]{0,1:T(8,128)(2,1)} %param.14), kind=kOutput, calls=%fused_computation.1 | convolution fusion | flops 663912 | bytes 679680 | tf_op jit(solution)/shard_map/dot_general | solution.py:120
  7.4 23.7 %all-gather.1 = f32[16,1,3456]{2,1,0:T(1,128)S(1)} all-gather(f32[1,1,3456]{2,1,0:T(1,128)S(1)} %convolution_bitcast_fusion), channel_id=2, replica_groups=mesh['req'=2,'patch'=16] {'patch'}, dimensions={0}, use_global_device_ids=true | all-gather | bytes 235008 | tf_op jit(solution)/shard_map/all_gather | solution.py:121
  31.3 4.6 %convolution_convert_fusion = bf16[48,3456]{1,0:T(8,128)(2,1)S(1)} fusion(bf16[1152,3456]{1,0:T(8,128)(2,1)} %param.16, f32[1152]{0:T(1024)S(1)} %get-tuple-element.6, f32[1152]{0:T(1024)S(1)} %get-tuple-element.7, f32[48]{0:T(128)S(1)} %add_rsqrt_fusion, f32[48]{0:T(128)S(1)} %broadcast_multiply_fusion, f32[48,1152]{1,0:T(8,128)S(1)} %concatenate.13, ...), kind=kOutput, calls=%fused_computation | convolution fusion | flops 382758912 | bytes 8635776 | tf_op jit(solution)/shard_map/dot_general | solution.py:134
  35.9 0.7 fusion.37
  37.0 0.7 copy.21
  37.7 3.5 %all-to-all-start = ((bf16[16,48,72]{2,1,0:T(8,128)(2,1)}), bf16[16,48,72]{2,1,0:T(8,128)(2,1)S(1)}, u32[]{:S(2)}, u32[]{:S(2)}) async-start(bf16[16,48,72]{2,1,0:T(8,128)(2,1)} %bitcast.40), calls=%async_computation | async-start | bytes 393216 | tf_op jit(solution)/shard_map/all_to_all | solution.py:149
  41.2 1.2 %reshape.177 = bf16[48,16,72]{2,1,0:T(8,128)(2,1)S(1)} reshape(bf16[48,1152]{1,0:T(8,128)(2,1)} %get-tuple-element.8) | data formatting | bytes 221184 | tf_op jit(solution)/shard_map/reshape | solution.py:141
  42.5 0.7 copy.16
  43.6 1.8 %maximum_bitcast_fusion = bf16[16,48,144]{2,1,0:T(8,128)(2,1)} fusion(bf16[48,16,72]{2,0,1:T(8,128)(2,1)S(1)} %copy.17, bf16[48,16,72]{2,0,1:T(8,128)(2,1)} %copy.16), kind=kLoop, calls=%fused_computation.18 | loop fusion | flops 442368 | bytes 442368 | tf_op jit(solution)/shard_map/transpose | solution.py:145
  45.4 4.7 %all-to-all-done = bf16[16,48,72]{2,1,0:T(8,128)(2,1)S(1)} async-done(((bf16[16,48,72]{2,1,0:T(8,128)(2,1)}), bf16[16,48,72]{2,1,0:T(8,128)(2,1)S(1)}, u32[]{:S(2)}, u32[]{:S(2)}) %all-to-all-start) | async-done | bytes 110624 | tf_op jit(solution)/shard_map/all_to_all | solution.py:149
  50.1 0.7 copy-done.2
  50.8 3.6 %all-to-all-start.1 = ((bf16[16,48,144]{2,1,0:T(8,128)(2,1)}), bf16[16,48,144]{2,1,0:T(8,128)(2,1)S(1)}, u32[]{:S(2)}, u32[]{:S(2)}) async-start(bf16[16,48,144]{2,1,0:T(8,128)(2,1)} %maximum_bitcast_fusion), calls=%async_computation.1 | async-start | bytes 786432 | tf_op jit(solution)/shard_map/all_to_all | solution.py:150
  54.5 12.0 %all-to-all-done.1 = bf16[16,48,144]{2,1,0:T(8,128)(2,1)S(1)} async-done(((bf16[16,48,144]{2,1,0:T(8,128)(2,1)}), bf16[16,48,144]{2,1,0:T(8,128)(2,1)S(1)}, u32[]{:S(2)}, u32[]{:S(2)}) %all-to-all-start.1) | async-done | bytes 221216 | tf_op jit(solution)/shard_map/all_to_all | solution.py:150
  66.5 1.5 %fusion.3 = (f32[768]{0:T(1024)S(1)}, f32[768,768]{0,1:T(8,128)S(1)}) fusion(pred[768]{0:T(1024)(128)(4,1)S(1)} %lt.37, bf16[768,72]{1,0:T(8,128)(2,1)} %bitcast.43, bf16[768,144]{1,0:T(8,128)(2,1)S(1)} %bitcast.41), kind=kOutput, calls=%fused_computation.8 | convolution fusion | flops 86703360 | bytes 2670592 | tf_op jit(solution)/shard_map/qhd,khd->hqk/dot_general | solution.py:37
  68.6 0.8 fusion.15
  69.5 0.8 copy.18
  70.3 3.5 %all-to-all-start.2 = ((bf16[16,48,72]{2,1,0:T(8,128)(2,1)}), bf16[16,48,72]{2,1,0:T(8,128)(2,1)S(1)}, u32[]{:S(2)}, u32[]{:S(2)}) async-start(bf16[16,48,72]{2,1,0:T(8,128)(2,1)} %bitcast.10), calls=%async_computation.2 | async-start | bytes 393216 | tf_op jit(solution)/shard_map/all_to_all | solution.py:163
  74.4 0.6 compare_convert_fusion
  75.0 7.7 %all-to-all-done.2 = bf16[16,48,72]{2,1,0:T(8,128)(2,1)S(1)} async-done(((bf16[16,48,72]{2,1,0:T(8,128)(2,1)}), bf16[16,48,72]{2,1,0:T(8,128)(2,1)S(1)}, u32[]{:S(2)}, u32[]{:S(2)}) %all-to-all-start.2) | async-done | bytes 110624 | tf_op jit(solution)/shard_map/all_to_all | solution.py:163
  83.0 1.2 %fusion.2 = bf16[48,1152]{1,0:T(8,128)(2,1)} fusion(bf16[48,1152]{1,0:T(8,128)(2,1)S(1)} %reshape.181, bf16[1152,1152]{1,0:T(8,128)(2,1)S(1)} %copy-done, f32[48]{0:T(128)S(1)} %compare_convert_fusion, f32[1152]{0:T(1024)S(1)} %get-tuple-element.5, f32[48,1152]{1,0:T(8,128)S(1)} %concatenate.13, bf16[48,1152]{1,0:T(8,128)(2,1)S(1)} %copy-done.1), kind=kOutput, calls=%fused_computation.7 | convolution fusion | flops 127733760 | bytes 3211968 | tf_op jit(solution)/shard_map/dot_general | solution.py:168
  (31 shorter events, 3.5 us)
Async XLA Ops:
  0.0 83.0 %copy-start = (bf16[1152,1152]{1,0:T(8,128)(2,1)S(1)}, bf16[1152,1152]{1,0:T(8,128)(2,1)}, u32[]{:S(2)}) copy-start(bf16[1152,1152]{1,0:T(8,128)(2,1)} %param.17) | copy-start | bytes 7962628
  0.0 31.3 %copy-start.1 = (bf16[48,1152]{1,0:T(8,128)(2,1)S(1)}, bf16[48,1152]{1,0:T(8,128)(2,1)}, u32[]{:S(2)}) copy-start(bf16[48,1152]{1,0:T(8,128)(2,1)} %param.9) | copy-start | bytes 331780
  35.9 18.4 %copy-start.3 = (s32[16]{0:T(128)S(1)}, s32[16]{0:T(128)}, u32[]{:S(2)}) copy-start(s32[16]{0:T(128)} %param.11) | copy-start | bytes 196
  37.7 12.5 %all-to-all-start = ((bf16[16,48,72]{2,1,0:T(8,128)(2,1)}), bf16[16,48,72]{2,1,0:T(8,128)(2,1)S(1)}, u32[]{:S(2)}, u32[]{:S(2)}) async-start(bf16[16,48,72]{2,1,0:T(8,128)(2,1)} %bitcast.40), calls=%async_computation | async-start | bytes 393216 | tf_op jit(solution)/shard_map/all_to_all | solution.py:149
  50.1 0.7 copy-start.2
  50.8 15.7 %all-to-all-start.1 = ((bf16[16,48,144]{2,1,0:T(8,128)(2,1)}), bf16[16,48,144]{2,1,0:T(8,128)(2,1)S(1)}, u32[]{:S(2)}, u32[]{:S(2)}) async-start(bf16[16,48,144]{2,1,0:T(8,128)(2,1)} %maximum_bitcast_fusion), calls=%async_computation.1 | async-start | bytes 786432 | tf_op jit(solution)/shard_map/all_to_all | solution.py:150
  70.3 12.5 %all-to-all-start.2 = ((bf16[16,48,72]{2,1,0:T(8,128)(2,1)}), bf16[16,48,72]{2,1,0:T(8,128)(2,1)S(1)}, u32[]{:S(2)}, u32[]{:S(2)}) async-start(bf16[16,48,72]{2,1,0:T(8,128)(2,1)} %bitcast.10), calls=%async_computation.2 | async-start | bytes 393216 | tf_op jit(solution)/shard_map/all_to_all | solution.py:163
